TPU v7x, 256 devices: a whole 4x4x8 slice. The times are simulated.
256 devices in a mesh: seqa: 16 (over x_hi, z), seqb: 16 (over x_lo, y, core).
Axes of the slice: x: 4 (x_hi: 2, x_lo: 2; x = x_hi * 2 + x_lo), y: 4, z: 8, core: 2. Of those that a mesh axis runs over, the one named last changes fastest.
Arguments:
- queries: bfloat16 [131072, 4096], P(('seqa', 'seqb')), may hold values from -60 to 60
- keys: bfloat16 [131072, 1024], P(('seqa', 'seqb')), may hold values from -8 to 8
- values: bfloat16 [131072, 1024], P(('seqa', 'seqb')), may hold values from -6 to 6
- doc_start: int32 [131072], P(('seqa', 'seqb')), may hold values from 0 to 131071, as said below
Outputs:
- attended: bfloat16 [131072, 4096], P(('seqa', 'seqb'))
Inputs may be any that keep to these rules, and one draw needn't show every extreme that they name: Never falling along the sequence, doc_start[i] <= i, the same value for all tokens of one document, and doc_start[0] = 0.
All inputs are finite; a program needn't handle non-finite values.
Results may differ from a plain program's by a relative error of at most 0.0038.
Values may be sent and summed in bfloat16 or wider, within the bound.
A program may use at most 64 MiB of HBM per device.

v0:
```python
import math

import jax
import jax.numpy as jnp
from jax import lax
from jax.sharding import PartitionSpec as P

HEAD_SIZE = 128


def passed_along(block, axis, distance):
    devices = range(lax.axis_size(axis))
    route = [(i - distance, i) for i in devices if i - distance in devices]
    return lax.ppermute(block, axis, route)


def attend_block(
    block_of_queries, block_of_keys, block_of_values, query_place, key_place, starts, window_length
):
    score_scale = 1.0 / math.sqrt(block_of_queries.shape[-1])
    scores = (
        jnp.einsum(
            "tgd,kd->gtk", block_of_queries, block_of_keys, preferred_element_type=jnp.float32
        )
        * score_scale
    )
    visible = (
        (key_place[None, :] <= query_place[:, None])
        & (key_place[None, :] > query_place[:, None] - window_length)
        & (key_place[None, :] >= starts[:, None])
    )
    scores = jnp.where(visible[None], scores, jnp.float32(-1e30))
    row_top = jnp.max(scores, axis=-1, keepdims=True)
    exponent = jnp.where(visible[None], jnp.exp(scores - row_top), jnp.float32(0.0))
    row_sum = jnp.sum(exponent, axis=-1, keepdims=True)
    weights = exponent.astype(jnp.bfloat16)
    summed = jnp.einsum("gtk,kd->tgd", weights, block_of_values, preferred_element_type=jnp.float32)
    return summed / jnp.transpose(row_sum, (1, 0, 2))


def local(queries, keys, values, doc_start):
    shard_rows = queries.shape[0]
    head_width = HEAD_SIZE
    group_width = queries.shape[1] // keys.shape[1]
    kv_heads = keys.shape[1] // head_width
    key_value = (keys, values)
    first_back = passed_along((key_value[0], key_value[1]), ("seqa", "seqb"), 1)
    second_back = passed_along((key_value[0], key_value[1]), ("seqa", "seqb"), 2)
    key_all = jnp.concatenate([second_back[0], first_back[0], keys], axis=0)
    value_all = jnp.concatenate([second_back[1], first_back[1], values], axis=0)
    window_length = 2 * shard_rows
    rows_per_block = min(512, shard_rows)
    block_count = shard_rows // rows_per_block
    shard_start = lax.axis_index(("seqa", "seqb")) * shard_rows

    def one_step(step_index, output):
        kv_head = step_index // block_count
        offset = step_index % block_count * rows_per_block
        block_of_queries = lax.dynamic_slice(
            queries,
            (offset, kv_head * group_width * head_width),
            (rows_per_block, group_width * head_width),
        )
        block_of_queries = block_of_queries.reshape(rows_per_block, group_width, head_width)
        block_of_keys = lax.dynamic_slice(
            key_all, (offset, kv_head * head_width), (window_length + rows_per_block, head_width)
        )
        block_of_values = lax.dynamic_slice(
            value_all, (offset, kv_head * head_width), (window_length + rows_per_block, head_width)
        )
        query_place = shard_start + offset + jnp.arange(rows_per_block, dtype=jnp.int32)
        key_place = (
            shard_start
            - window_length
            + offset
            + jnp.arange(window_length + rows_per_block, dtype=jnp.int32)
        )
        attended_block = attend_block(
            block_of_queries,
            block_of_keys,
            block_of_values,
            query_place,
            key_place,
            doc_start,
            window_length,
        )
        attended_block = attended_block.reshape(rows_per_block, group_width * head_width).astype(
            jnp.bfloat16
        )
        return lax.dynamic_update_slice(
            output, attended_block, (offset, kv_head * group_width * head_width)
        )

    return lax.fori_loop(0, kv_heads * block_count, one_step, jnp.zeros_like(queries))


def solution(mesh):
    return jax.shard_map(
        local,
        mesh=mesh,
        in_specs=(
            P(("seqa", "seqb"), None),
            P(("seqa", "seqb"), None),
            P(("seqa", "seqb"), None),
            P(("seqa", "seqb")),
        ),
        out_specs=P(("seqa", "seqb"), None),
        check_vma=False,
    )
```

profile of v0, /device:TPU:4, one launch (start us, length us, event | category | flops | bytes accessed | tf_op | source)
XLA Modules:
  0.0 216.3 jit_solution(11983723180137291054)
XLA Ops:
  3.5 3.5 %collective-permute-start = (bf16[512,1024]{0,1:T(8,128)(2,1)S(1)}, bf16[512,1024]{0,1:T(8,128)(2,1)}, u32[]{:S(2)}, u32[]{:S(2)}) collective-permute-start(bf16[512,1024]{0,1:T(8,128)(2,1)S(1)} %copy.12), channel_id=1, source_target_pairs={{0,2},{1,3},{2,4},{3,5},{4,6},{5,7},{6,8},{7,9},{8,10},{9,11},{10,... | collective-permute-start | bytes 3145736 | tf_op jit(solution)/shard_map/ppermute | solution.py:14
  7.0 3.5 %collective-permute-start.2 = (bf16[512,1024]{1,0:T(8,128)(2,1)}, bf16[512,1024]{1,0:T(8,128)(2,1)S(1)}, u32[]{:S(2)}, u32[]{:S(2)}) collective-permute-start(bf16[512,1024]{1,0:T(8,128)(2,1)} %param.7), channel_id=1, source_target_pairs={{0,2},{1,3},{2,4},{3,5},{4,6},{5,7},{6,8},{7,9},{8,10},{9,11},{10,... | collective-permute-start | bytes 3145736 | tf_op jit(solution)/shard_map/ppermute | solution.py:14
  13.3 19.0 %collective-permute-done.1 = bf16[512,1024]{0,1:T(8,128)(2,1)} collective-permute-done((bf16[512,1024]{0,1:T(8,128)(2,1)S(1)}, bf16[512,1024]{0,1:T(8,128)(2,1)}, u32[]{:S(2)}, u32[]{:S(2)}) %collective-permute-start.1) | collective-permute-done | bytes 1048608 | tf_op jit(solution)/shard_map/ppermute | solution.py:14
  32.2 5.6 %collective-permute-done = bf16[512,1024]{0,1:T(8,128)(2,1)} collective-permute-done((bf16[512,1024]{0,1:T(8,128)(2,1)S(1)}, bf16[512,1024]{0,1:T(8,128)(2,1)}, u32[]{:S(2)}, u32[]{:S(2)}) %collective-permute-start) | collective-permute-done | bytes 1048608 | tf_op jit(solution)/shard_map/ppermute | solution.py:14
  37.8 3.0 %pad_maximum_fusion = bf16[1536,1024]{0,1:T(8,128)(2,1)} fusion(bf16[512,1024]{0,1:T(8,128)(2,1)S(1)} %copy.12, bf16[512,1024]{0,1:T(8,128)(2,1)} %collective-permute-done.1, bf16[512,1024]{0,1:T(8,128)(2,1)} %collective-permute-done), kind=kLoop, calls=%fused_computation.31 | loop fusion | flops 9437184 | bytes 6291456 | tf_op jit(solution)/shard_map/concatenate | solution.py:50
  40.8 19.4 %collective-permute-done.2 = bf16[512,1024]{1,0:T(8,128)(2,1)S(1)} collective-permute-done((bf16[512,1024]{1,0:T(8,128)(2,1)}, bf16[512,1024]{1,0:T(8,128)(2,1)S(1)}, u32[]{:S(2)}, u32[]{:S(2)}) %collective-permute-start.2) | collective-permute-done | bytes 1048608 | tf_op jit(solution)/shard_map/ppermute | solution.py:14
  60.2 19.8 %collective-permute-done.3 = bf16[512,1024]{1,0:T(8,128)(2,1)} collective-permute-done((bf16[512,1024]{1,0:T(8,128)(2,1)}, bf16[512,1024]{1,0:T(8,128)(2,1)}, u32[]{:S(2)}, u32[]{:S(2)}) %collective-permute-start.3) | collective-permute-done | bytes 1048608 | tf_op jit(solution)/shard_map/ppermute | solution.py:14
  85.4 131.0 %while.16 = (s32[]{:T(128)}, bf16[512,4096]{1,0:T(8,128)(2,1)}, bf16[1536,1024]{0,1:T(8,128)(2,1)}, s32[]{:T(128)}, s32[]{:T(128)}, /*index=5*/s32[512]{0:T(512)...) while((s32[]{:T(128)}, bf16[512,4096]{1,0:T(8,128)(2,1)}, ...), condition=%wide.region_3.4_spmd, body=%wide.region_0.3_spmd.sunk | while | flops 1633947648 | bytes 21010688 | solution.py:94
  87.8 8.9 %fusion.56 = (f32[4,512]{1,0:T(4,128)S(1)}, bf16[4,512,1536]{1,2,0:T(8,128)(2,1)}) fusion(pred[512,1536]{0,1:T(8,128)(4,1)S(1)} %compare_and_fusion.2, bf16[512,4,128]{0,2,1:T(8,128)(2,1)S(1)} %bitcast.61, bf16[1536,1024]{1,0:T(8,128)(2,1)} %get-tuple-element.346, s32[]{:T(128)S(6)} %select_n.95), kind=kOutput, calls=%fused_computation.33.clone.1 | convolution fusion | flops 824182272 | bytes 8790020 | tf_op jit(solution)/shard_map/while/body/eval_jaxpr/sub | solution.py:34
  96.8 3.9 %fusion.57 = bf16[512,4,128]{0,2,1:T(8,128)(2,1)S(1)} fusion(bf16[4,512,1536]{1,2,0:T(8,128)(2,1)} %get-tuple-element.310, f32[512,4]{0,1:T(4,128)S(1)} %bitcast.63, bf16[1536,1024]{0,1:T(8,128)(2,1)} %get-tuple-element.342, s32[]{:T(128)S(6)} %select_n.95), kind=kOutput, calls=%fused_computation.13.clone.1 | convolution fusion | flops 805830656 | bytes 7217156 | tf_op jit(solution)/shard_map/while/body/eval_jaxpr/gtk,kd->tgd/dot_general | solution.py:37
  104.2 8.9 %fusion.56 = (f32[4,512]{1,0:T(4,128)S(1)}, bf16[4,512,1536]{1,2,0:T(8,128)(2,1)}) fusion(pred[512,1536]{0,1:T(8,128)(4,1)S(1)} %compare_and_fusion.2, bf16[512,4,128]{0,2,1:T(8,128)(2,1)S(1)} %bitcast.61, bf16[1536,1024]{1,0:T(8,128)(2,1)} %get-tuple-element.346, s32[]{:T(128)S(6)} %select_n.95), kind=kOutput, calls=%fused_computation.33.clone.1 | convolution fusion | flops 824182272 | bytes 8790020 | tf_op jit(solution)/shard_map/while/body/eval_jaxpr/sub | solution.py:34
  113.1 3.9 %fusion.57 = bf16[512,4,128]{0,2,1:T(8,128)(2,1)S(1)} fusion(bf16[4,512,1536]{1,2,0:T(8,128)(2,1)} %get-tuple-element.310, f32[512,4]{0,1:T(4,128)S(1)} %bitcast.63, bf16[1536,1024]{0,1:T(8,128)(2,1)} %get-tuple-element.342, s32[]{:T(128)S(6)} %select_n.95), kind=kOutput, calls=%fused_computation.13.clone.1 | convolution fusion | flops 805830656 | bytes 7217156 | tf_op jit(solution)/shard_map/while/body/eval_jaxpr/gtk,kd->tgd/dot_general | solution.py:37
  120.6 8.9 %fusion.56 = (f32[4,512]{1,0:T(4,128)S(1)}, bf16[4,512,1536]{1,2,0:T(8,128)(2,1)}) fusion(pred[512,1536]{0,1:T(8,128)(4,1)S(1)} %compare_and_fusion.2, bf16[512,4,128]{0,2,1:T(8,128)(2,1)S(1)} %bitcast.61, bf16[1536,1024]{1,0:T(8,128)(2,1)} %get-tuple-element.346, s32[]{:T(128)S(6)} %select_n.95), kind=kOutput, calls=%fused_computation.33.clone.1 | convolution fusion | flops 824182272 | bytes 8790020 | tf_op jit(solution)/shard_map/while/body/eval_jaxpr/sub | solution.py:34
  129.5 3.9 %fusion.57 = bf16[512,4,128]{0,2,1:T(8,128)(2,1)S(1)} fusion(bf16[4,512,1536]{1,2,0:T(8,128)(2,1)} %get-tuple-element.310, f32[512,4]{0,1:T(4,128)S(1)} %bitcast.63, bf16[1536,1024]{0,1:T(8,128)(2,1)} %get-tuple-element.342, s32[]{:T(128)S(6)} %select_n.95), kind=kOutput, calls=%fused_computation.13.clone.1 | convolution fusion | flops 805830656 | bytes 7217156 | tf_op jit(solution)/shard_map/while/body/eval_jaxpr/gtk,kd->tgd/dot_general | solution.py:37
  137.0 8.9 %fusion.56 = (f32[4,512]{1,0:T(4,128)S(1)}, bf16[4,512,1536]{1,2,0:T(8,128)(2,1)}) fusion(pred[512,1536]{0,1:T(8,128)(4,1)S(1)} %compare_and_fusion.2, bf16[512,4,128]{0,2,1:T(8,128)(2,1)S(1)} %bitcast.61, bf16[1536,1024]{1,0:T(8,128)(2,1)} %get-tuple-element.346, s32[]{:T(128)S(6)} %select_n.95), kind=kOutput, calls=%fused_computation.33.clone.1 | convolution fusion | flops 824182272 | bytes 8790020 | tf_op jit(solution)/shard_map/while/body/eval_jaxpr/sub | solution.py:34
  145.9 3.9 %fusion.57 = bf16[512,4,128]{0,2,1:T(8,128)(2,1)S(1)} fusion(bf16[4,512,1536]{1,2,0:T(8,128)(2,1)} %get-tuple-element.310, f32[512,4]{0,1:T(4,128)S(1)} %bitcast.63, bf16[1536,1024]{0,1:T(8,128)(2,1)} %get-tuple-element.342, s32[]{:T(128)S(6)} %select_n.95), kind=kOutput, calls=%fused_computation.13.clone.1 | convolution fusion | flops 805830656 | bytes 7217156 | tf_op jit(solution)/shard_map/while/body/eval_jaxpr/gtk,kd->tgd/dot_general | solution.py:37
  153.3 8.9 %fusion.56 = (f32[4,512]{1,0:T(4,128)S(1)}, bf16[4,512,1536]{1,2,0:T(8,128)(2,1)}) fusion(pred[512,1536]{0,1:T(8,128)(4,1)S(1)} %compare_and_fusion.2, bf16[512,4,128]{0,2,1:T(8,128)(2,1)S(1)} %bitcast.61, bf16[1536,1024]{1,0:T(8,128)(2,1)} %get-tuple-element.346, s32[]{:T(128)S(6)} %select_n.95), kind=kOutput, calls=%fused_computation.33.clone.1 | convolution fusion | flops 824182272 | bytes 8790020 | tf_op jit(solution)/shard_map/while/body/eval_jaxpr/sub | solution.py:34
  162.2 3.9 %fusion.57 = bf16[512,4,128]{0,2,1:T(8,128)(2,1)S(1)} fusion(bf16[4,512,1536]{1,2,0:T(8,128)(2,1)} %get-tuple-element.310, f32[512,4]{0,1:T(4,128)S(1)} %bitcast.63, bf16[1536,1024]{0,1:T(8,128)(2,1)} %get-tuple-element.342, s32[]{:T(128)S(6)} %select_n.95), kind=kOutput, calls=%fused_computation.13.clone.1 | convolution fusion | flops 805830656 | bytes 7217156 | tf_op jit(solution)/shard_map/while/body/eval_jaxpr/gtk,kd->tgd/dot_general | solution.py:37
  169.7 8.9 %fusion.56 = (f32[4,512]{1,0:T(4,128)S(1)}, bf16[4,512,1536]{1,2,0:T(8,128)(2,1)}) fusion(pred[512,1536]{0,1:T(8,128)(4,1)S(1)} %compare_and_fusion.2, bf16[512,4,128]{0,2,1:T(8,128)(2,1)S(1)} %bitcast.61, bf16[1536,1024]{1,0:T(8,128)(2,1)} %get-tuple-element.346, s32[]{:T(128)S(6)} %select_n.95), kind=kOutput, calls=%fused_computation.33.clone.1 | convolution fusion | flops 824182272 | bytes 8790020 | tf_op jit(solution)/shard_map/while/body/eval_jaxpr/sub | solution.py:34
  178.6 3.9 %fusion.57 = bf16[512,4,128]{0,2,1:T(8,128)(2,1)S(1)} fusion(bf16[4,512,1536]{1,2,0:T(8,128)(2,1)} %get-tuple-element.310, f32[512,4]{0,1:T(4,128)S(1)} %bitcast.63, bf16[1536,1024]{0,1:T(8,128)(2,1)} %get-tuple-element.342, s32[]{:T(128)S(6)} %select_n.95), kind=kOutput, calls=%fused_computation.13.clone.1 | convolution fusion | flops 805830656 | bytes 7217156 | tf_op jit(solution)/shard_map/while/body/eval_jaxpr/gtk,kd->tgd/dot_general | solution.py:37
  186.1 8.9 %fusion.56 = (f32[4,512]{1,0:T(4,128)S(1)}, bf16[4,512,1536]{1,2,0:T(8,128)(2,1)}) fusion(pred[512,1536]{0,1:T(8,128)(4,1)S(1)} %compare_and_fusion.2, bf16[512,4,128]{0,2,1:T(8,128)(2,1)S(1)} %bitcast.61, bf16[1536,1024]{1,0:T(8,128)(2,1)} %get-tuple-element.346, s32[]{:T(128)S(6)} %select_n.95), kind=kOutput, calls=%fused_computation.33.clone.1 | convolution fusion | flops 824182272 | bytes 8790020 | tf_op jit(solution)/shard_map/while/body/eval_jaxpr/sub | solution.py:34
  195.0 3.9 %fusion.57 = bf16[512,4,128]{0,2,1:T(8,128)(2,1)S(1)} fusion(bf16[4,512,1536]{1,2,0:T(8,128)(2,1)} %get-tuple-element.310, f32[512,4]{0,1:T(4,128)S(1)} %bitcast.63, bf16[1536,1024]{0,1:T(8,128)(2,1)} %get-tuple-element.342, s32[]{:T(128)S(6)} %select_n.95), kind=kOutput, calls=%fused_computation.13.clone.1 | convolution fusion | flops 805830656 | bytes 7217156 | tf_op jit(solution)/shard_map/while/body/eval_jaxpr/gtk,kd->tgd/dot_general | solution.py:37
  202.4 8.9 %fusion.56 = (f32[4,512]{1,0:T(4,128)S(1)}, bf16[4,512,1536]{1,2,0:T(8,128)(2,1)}) fusion(pred[512,1536]{0,1:T(8,128)(4,1)S(1)} %compare_and_fusion.2, bf16[512,4,128]{0,2,1:T(8,128)(2,1)S(1)} %bitcast.61, bf16[1536,1024]{1,0:T(8,128)(2,1)} %get-tuple-element.346, s32[]{:T(128)S(6)} %select_n.95), kind=kOutput, calls=%fused_computation.33.clone.1 | convolution fusion | flops 824182272 | bytes 8790020 | tf_op jit(solution)/shard_map/while/body/eval_jaxpr/sub | solution.py:34
  211.4 3.9 %fusion.57 = bf16[512,4,128]{0,2,1:T(8,128)(2,1)S(1)} fusion(bf16[4,512,1536]{1,2,0:T(8,128)(2,1)} %get-tuple-element.310, f32[512,4]{0,1:T(4,128)S(1)} %bitcast.63, bf16[1536,1024]{0,1:T(8,128)(2,1)} %get-tuple-element.342, s32[]{:T(128)S(6)} %select_n.95), kind=kOutput, calls=%fused_computation.13.clone.1 | convolution fusion | flops 805830656 | bytes 7217156 | tf_op jit(solution)/shard_map/while/body/eval_jaxpr/gtk,kd->tgd/dot_general | solution.py:37
  (65 shorter events, 39.6 us)
Async XLA Ops:
  0.0 80.0 %copy-start = (bf16[512,1024]{1,0:T(8,128)(2,1)S(1)}, bf16[512,1024]{1,0:T(8,128)(2,1)}, u32[]{:S(2)}) copy-start(bf16[512,1024]{1,0:T(8,128)(2,1)} %param.7) | copy-start | bytes 3145732
  1.6 30.7 %collective-permute-start.1 = (bf16[512,1024]{0,1:T(8,128)(2,1)S(1)}, bf16[512,1024]{0,1:T(8,128)(2,1)}, u32[]{:S(2)}, u32[]{:S(2)}) collective-permute-start(bf16[512,1024]{0,1:T(8,128)(2,1)S(1)} %copy.12), channel_id=1, source_target_pairs={{0,1},{1,2},{2,3},{3,4},{4,5},{5,6},{6,7},{7,8},{8,9},{9,10},{10,1... | collective-permute-start | bytes 3145736 | tf_op jit(solution)/shard_map/ppermute | solution.py:14
  3.5 34.3 %collective-permute-start = (bf16[512,1024]{0,1:T(8,128)(2,1)S(1)}, bf16[512,1024]{0,1:T(8,128)(2,1)}, u32[]{:S(2)}, u32[]{:S(2)}) collective-permute-start(bf16[512,1024]{0,1:T(8,128)(2,1)S(1)} %copy.12), channel_id=1, source_target_pairs={{0,2},{1,3},{2,4},{3,5},{4,6},{5,7},{6,8},{7,9},{8,10},{9,11},{10,... | collective-permute-start | bytes 3145736 | tf_op jit(solution)/shard_map/ppermute | solution.py:14
  7.0 53.2 %collective-permute-start.2 = (bf16[512,1024]{1,0:T(8,128)(2,1)}, bf16[512,1024]{1,0:T(8,128)(2,1)S(1)}, u32[]{:S(2)}, u32[]{:S(2)}) collective-permute-start(bf16[512,1024]{1,0:T(8,128)(2,1)} %param.7), channel_id=1, source_target_pairs={{0,2},{1,3},{2,4},{3,5},{4,6},{5,7},{6,8},{7,9},{8,10},{9,11},{10,... | collective-permute-start | bytes 3145736 | tf_op jit(solution)/shard_map/ppermute | solution.py:14
  10.5 69.5 %collective-permute-start.3 = (bf16[512,1024]{1,0:T(8,128)(2,1)}, bf16[512,1024]{1,0:T(8,128)(2,1)}, u32[]{:S(2)}, u32[]{:S(2)}) collective-permute-start(bf16[512,1024]{1,0:T(8,128)(2,1)} %param.7), channel_id=1, source_target_pairs={{0,1},{1,2},{2,3},{3,4},{4,5},{5,6},{6,7},{7,8},{8,9},{9,10},{10,1... | collective-permute-start | bytes 3145736 | tf_op jit(solution)/shard_map/ppermute | solution.py:14
  40.8 44.5 %copy-start.1 = (s32[512]{0:T(512)S(1)}, s32[512]{0:T(512)}, u32[]{:S(2)}) copy-start(s32[512]{0:T(512)} %param.9) | copy-start | bytes 6148
where the time goes:
time: 217 us; the launch traced here: 216 us
  matrix products  103 us (47%)
  waiting for transfers between devices  63.7 us (29%)
  local copies, waits for them, and re-layouts  22.8 us (11%)
  other arithmetic  15.2 us (7%)
  starting transfers between devices  11.6 us (5%)
    sub x8, matrix products, attend_block(): scores - row_top  71.3 us
    ppermute x4, waiting for transfers between devices, passed_along(): return lax.ppermute(block, axis, route)  63.7 us
    dot_general x8, matrix products, attend_block(): jnp.einsum('gtk,kd->tgd', weights, block_of_values, preferred_element_typ...  31.4 us
    ppermute x4, starting transfers between devices, passed_along(): return lax.ppermute(block, axis, route)  11.6 us
    dynamic_slice x16, local copies, waits for them, and re-layouts, one_step(): lax.dynamic_slice(queries, (offset, kv_head * group_width * head_width),...  10.3 us
    and x8, other arithmetic, attend_block(): (key_place[None, :] <= query_place[:, None]) & (key_place[None, :] > quer...  9.27 us
    dynamic_update_slice x16, local copies, waits for them, and re-layouts, one_step(): lax.dynamic_update_slice(output, attended_block, (offset, kv_head * group...  8.37 us
  transfers between devices with their start and end apart: 4, of which 4 were waited for; matrix products, arithmetic and copies ran while one was open for 1% of the time, Pallas kernels for 0%

commit v1 on v0

v1 whole, which is shorter than its diff:
```python
import functools
import math

import jax
import jax.numpy as jnp
from jax import lax
from jax.experimental import pallas as pl
from jax.experimental.pallas import tpu as pltpu
from jax.sharding import PartitionSpec as P

MESH = pl.DeviceIdType.MESH
HEAD = 128
ROWS = 512
BLOCK = 256
SPAN = 5 * BLOCK
SCALE = math.log2(math.e) / math.sqrt(HEAD)
ROUND = (4, 7)
COLUMN = 4


def places(chips):
    seqb = lax.axis_index("seqb")
    wide = lax.axis_size("seqb") // 2
    chip = lax.axis_index("seqa") * wide + seqb // 2
    core = lax.rem(seqb, 2)
    y = lax.rem(chip, COLUMN)

    def at(chip_index, core_index=core):
        return (chip_index // wide, lax.rem(chip_index, wide) * 2 + core_index)

    def in_column(chip_index, step):
        place = lax.rem(chip_index, COLUMN)
        return chip_index - place + lax.rem(place + step, COLUMN)

    before = lax.rem(chip + chips - 1, chips)
    return dict(
        core=core,
        partner=at(chip, 1 - core),
        after=at(lax.rem(chip + 1, chips)),
        before=at(before),
        down=at(in_column(chip, 3)),
        up=at(in_column(chip, 1)),
        last_to=at(lax.rem(in_column(chip, 2) + 1, chips)),
        last_from=at(in_column(before, 2)),
    )


def attend(head, q_ref, kv, bias, scores, weights, out, block):
    rows = slice(block * BLOCK, (block + 1) * BLOCK)
    keys = block * BLOCK
    for g in range(4):
        unit = (block * 4 + g) % 2
        s_ref, w_ref = scores.at[unit], weights.at[unit]
        columns = pl.ds(pl.multiple_of(head * 4 * HEAD, 4 * HEAD) + g * HEAD, HEAD)
        q = q_ref[rows, columns]
        top = None
        for t in range(5):
            span = slice(t * BLOCK, (t + 1) * BLOCK)
            k = kv[head, 0, keys + t * BLOCK : keys + (t + 1) * BLOCK, :]
            s = lax.dot_general(
                q, k, (((1,), (1,)), ((), ())), preferred_element_type=jnp.float32
            )
            s = jnp.minimum(s, bias[block, :, span])
            s_ref[:, span] = s
            s = jnp.maximum(s[:, :HEAD], s[:, HEAD:])
            top = s if top is None else jnp.maximum(top, s)
        top = jnp.max(top, axis=1, keepdims=True)
        for t in range(5):
            span = slice(t * BLOCK, (t + 1) * BLOCK)
            w = jnp.exp2((s_ref[:, span] - top) * SCALE)
            w_ref[:, span] = w.astype(jnp.bfloat16)
        v = kv[head, 1, keys : keys + SPAN, :]
        v = jnp.concatenate([v, jnp.ones((SPAN, HEAD), jnp.bfloat16)], axis=1)
        o = jnp.dot(w_ref[...], v, preferred_element_type=jnp.float32)
        o = o[:, :HEAD] / o[:, HEAD:]
        out[rows, columns] = o.astype(jnp.bfloat16)


def kernel(
    chips, q_hbm, k_hbm, v_hbm, start_ref, o_hbm,
    q_ref, kv, hop, bias, scores, weights, out,
    kv_sem, q_sem, o_sem, far_send, far_recv, near_send, near_recv, hop_send, hop_recv,
):
    heads = kv.shape[0]
    at = places(chips)
    own, one, two = slice(1024, 1536), slice(512, 1024), slice(0, 512)

    def load_kv(h, which):
        src = (k_hbm, v_hbm)[which]
        return pltpu.make_async_copy(
            src.at[:, pl.ds(h * HEAD, HEAD)], kv.at[h, which, own], kv_sem.at[h, which]
        )

    def load_q(h):
        columns = pl.ds(pl.multiple_of(h * 4 * HEAD, 4 * HEAD), 4 * HEAD)
        return pltpu.make_async_copy(q_hbm.at[:, columns], q_ref.at[:, columns], q_sem.at[h])

    def store_o(h):
        columns = pl.ds(pl.multiple_of(h * 4 * HEAD, 4 * HEAD), 4 * HEAD)
        return pltpu.make_async_copy(out.at[:, columns], o_hbm.at[:, columns], o_sem.at[h])

    def far(h):
        return pltpu.make_async_remote_copy(
            kv.at[h, :, own], kv.at[h, :, two], far_send.at[h], far_recv.at[h],
            device_id=at["after"], device_id_type=MESH,
        )

    def near(h, src):
        return pltpu.make_async_remote_copy(
            kv.at[h, :, src], kv.at[h, :, one], near_send.at[h], near_recv.at[h],
            device_id=at["partner"], device_id_type=MESH,
        )

    def first_hop(i):
        return pltpu.make_async_remote_copy(
            kv.at[ROUND[i], :, own], hop.at[0, i], hop_send.at[0, i], hop_recv.at[0, i],
            device_id=at["down"], device_id_type=MESH,
        )

    def second_hop(i):
        return pltpu.make_async_remote_copy(
            hop.at[0, i], hop.at[1, i], hop_send.at[1, i], hop_recv.at[1, i],
            device_id=at["down"], device_id_type=MESH,
        )

    def third_hop(i):
        h = ROUND[i]
        return pltpu.make_async_remote_copy(
            hop.at[1, i], kv.at[h, :, two], far_send.at[h], far_recv.at[h],
            device_id=at["last_to"], device_id_type=MESH,
        )

    order = [0, ROUND[0]] + [h for h in range(1, heads) if h not in (ROUND[0],)]
    for h in order:
        for which in range(2):
            load_kv(h, which).start()
    for h in range(heads):
        load_q(h).start()

    barrier = pltpu.get_barrier_semaphore()
    peers = ("partner", "after", "before", "down", "up", "last_to", "last_from")
    for name in peers:
        pl.semaphore_signal(barrier, inc=1, device_id=at[name], device_id_type=MESH)

    shard = lax.axis_index("seqa") * lax.axis_size("seqb") + lax.axis_index("seqb")
    for block in range(2):
        starts = []
        for r in range(2):
            row = start_ref[pl.ds(block * 2 + r, 1), :] - shard * ROWS
            row = jnp.broadcast_to(row.astype(jnp.float32), (HEAD, HEAD))
            starts.append(row.T)
        start = jnp.concatenate(starts, axis=0)
        for t in range(SPAN // HEAD):
            q_place = lax.broadcasted_iota(jnp.int32, (BLOCK, HEAD), 0) + block * BLOCK
            k_place = lax.broadcasted_iota(jnp.int32, (BLOCK, HEAD), 1) + (
                t * HEAD + block * BLOCK - 2 * ROWS
            )
            seen = (
                (k_place <= q_place)
                & (k_place > q_place - 2 * ROWS)
                & (k_place.astype(jnp.float32) >= start)
            )
            bias[block, :, t * HEAD : (t + 1) * HEAD] = jnp.where(
                seen, jnp.float32(3e38), jnp.float32(-1e30)
            )

    pl.semaphore_wait(barrier, len(peers))

    for h in order:
        for which in range(2):
            load_kv(h, which).wait()
        if h in ROUND:
            first_hop(ROUND.index(h)).start()
        else:
            far(h).start()

        @pl.when(at["core"] == 0)
        def _():
            near(h, own).start()

    def step(h, carry):
        for i in range(2):

            @pl.when(h == i)
            def _():
                first_hop(i).wait_recv()
                second_hop(i).start()

            @pl.when(h == 2 + i)
            def _():
                second_hop(i).wait_recv()
                third_hop(i).start()

        far(h).wait_recv()

        @pl.when(at["core"] == 1)
        def _():
            near(h, two).start()

        load_q(h).wait()
        near(h, own).wait_recv()
        for block in range(2):
            attend(h, q_ref, kv, bias, scores, weights, out, block)
        store_o(h).start()
        return carry

    lax.fori_loop(0, heads, step, 0)

    for h in range(heads):
        store_o(h).wait()
        near(h, own).wait_send()
        if h not in ROUND:
            far(h).wait_send()
    for i in range(2):
        first_hop(i).wait_send()
        second_hop(i).wait_send()
        third_hop(i).wait_send()


def local(queries, keys, values, doc_start):
    heads = keys.shape[1] // HEAD
    chips = lax.axis_size("seqa") * lax.axis_size("seqb") // 2
    anywhere = pl.BlockSpec(memory_space=pl.ANY)
    dma = pltpu.SemaphoreType.DMA
    return pl.pallas_call(
        functools.partial(kernel, chips),
        out_shape=jax.ShapeDtypeStruct(queries.shape, queries.dtype),
        in_specs=[anywhere] * 3 + [pl.BlockSpec(memory_space=pltpu.VMEM)],
        out_specs=anywhere,
        scratch_shapes=[
            pltpu.VMEM(queries.shape, jnp.bfloat16),
            pltpu.VMEM((heads, 2, 3 * ROWS, HEAD), jnp.bfloat16),
            pltpu.VMEM((2, 2, 2, ROWS, HEAD), jnp.bfloat16),
            pltpu.VMEM((2, BLOCK, SPAN), jnp.float32),
            pltpu.VMEM((2, BLOCK, SPAN), jnp.float32),
            pltpu.VMEM((2, BLOCK, SPAN), jnp.bfloat16),
            pltpu.VMEM(queries.shape, jnp.bfloat16),
            dma((heads, 2)), dma((heads,)), dma((heads,)),
            dma((heads,)), dma((heads,)), dma((heads,)), dma((heads,)),
            dma((2, 2)), dma((2, 2)),
        ],
        compiler_params=pltpu.CompilerParams(
            collective_id=0, has_side_effects=True, vmem_limit_bytes=60 * 2**20
        ),
        name="attention",
    )(queries, keys, values, doc_start.reshape(ROWS // HEAD, HEAD))


def solution(mesh):
    shards = P(("seqa", "seqb"), None)
    return jax.shard_map(
        local,
        mesh=mesh,
        in_specs=(shards, shards, shards, P(("seqa", "seqb"))),
        out_specs=shards,
        check_vma=False,
    )
```

time: 217 us -> 65.5 us (0.30)
  the two profiles are of different devices: /device:TPU:4 before, /device:TPU:102 now
where the time goes in v1:
time: 65.5 us; the launch traced here: 65.4 us
  Pallas kernels  60.7 us (93%)
  local copies, waits for them, and re-layouts  4.7 us (7%)
    pallas_call x1, Pallas kernels, local(): pl.pallas_call(functools.partial(kernel, chips), out_shape=jax.ShapeDtype...  60.7 us
    unnamed x1, local copies, waits for them, and re-layouts  4.7 us

profile of v1, /device:TPU:102, one launch (start us, length us, event | category | flops | bytes accessed | tf_op | source)
XLA Modules:
  0.0 65.4 jit_solution(4352425888560601849)
XLA Ops:
  0.0 60.7 %attention.1 = bf16[512,4096]{1,0:T(8,128)(2,1)} custom-call(bf16[512,4096]{1,0:T(8,128)(2,1)} %q_hbm.1, bf16[512,1024]{1,0:T(8,128)(2,1)} %k_hbm.1, bf16[512,1024]{1,0:T(8,128)(2,1)} %v_hbm.1, s32[4,128]{1,0:T(4,128)} %bitcast.1), custom_call_target="tpu_custom_call" | custom-call | tf_op jit(solution)/shard_map/attention/pallas_call | solution.py:225
  60.7 4.7 %copy.6 = bf16[512,4096]{1,0:T(8,128)(2,1)} copy(bf16[512,4096]{1,0:T(8,128)(2,1)} %attention.1) | data formatting | bytes 8388608

commit v2 on v1

v2 whole, which is shorter than its diff:
```python
import functools
import math

import jax
import jax.numpy as jnp
from jax import lax
from jax.experimental import pallas as pl
from jax.experimental.pallas import tpu as pltpu
from jax.sharding import PartitionSpec as P

MESH = pl.DeviceIdType.MESH
HEAD = 128
ROWS = 512
BLOCK = 256
SPAN = 5 * BLOCK
SCALE = math.log2(math.e) / math.sqrt(HEAD)
ROUND = ((4, 0), (4, 1), (7, 0))
LAST = 7
COLUMN = 4


def places(chips):
    seqb = lax.axis_index("seqb")
    wide = lax.axis_size("seqb") // 2
    chip = lax.axis_index("seqa") * wide + seqb // 2
    core = lax.rem(seqb, 2)

    def at(chip_index, core_index=core):
        return (chip_index // wide, lax.rem(chip_index, wide) * 2 + core_index)

    def in_column(chip_index, step):
        place = lax.rem(chip_index, COLUMN)
        return chip_index - place + lax.rem(place + step, COLUMN)

    before = lax.rem(chip + chips - 1, chips)
    return dict(
        core=core,
        partner=at(chip, 1 - core),
        after=at(lax.rem(chip + 1, chips)),
        before=at(before),
        down=at(in_column(chip, 3)),
        up=at(in_column(chip, 1)),
        last_to=at(lax.rem(in_column(chip, 2) + 1, chips)),
        last_from=at(in_column(before, 2)),
        has_before=chip != 0,
        peers=4 - (chip + 1) // chips - (in_column(chip, 2) + 1) // chips,
        has_after=chip != chips - 1,
        has_last_to=in_column(chip, 2) != chips - 1,
    )


def scaled(x):
    return jnp.exp2(x * SCALE)


def attend(head, slot, q_ref, kv, bias, scores, weights, state, out, blocks, part, between=None):
    units = [(block, g) for block in blocks for g in range(4)]
    tops = {}

    def span_of(block):
        first = 2 * ROWS if part == "own" else block * BLOCK
        last = 2 * ROWS if part == "before" else block * BLOCK + SPAN
        return first, last, range(first, last, BLOCK)

    def place(block, g):
        columns = pl.ds(slot * 4 * HEAD + g * HEAD, HEAD)
        return slice(block * BLOCK, (block + 1) * BLOCK), columns

    def score(n, x):
        block, g = units[n]
        first, last, _ = span_of(block)
        span, seen = (slice(x - y, x - y + BLOCK) for y in (first, block * BLOCK))
        k = kv[slot, 0, x : x + BLOCK, :]
        s = lax.dot_general(
            q_ref[place(block, g)], k, (((1,), (1,)), ((), ())), preferred_element_type=jnp.float32
        )
        s = jnp.minimum(s, bias[block, :, seen])
        scores[n % 2, :, span] = s
        s = jnp.maximum(s[:, :HEAD], s[:, HEAD:])
        if x > first:
            s = jnp.maximum(s, tops[n])
        elif part == "before":
            s = jnp.maximum(s, state[2][head, block * 4 + g])
        tops[n] = jnp.max(s, axis=1, keepdims=True) if x + BLOCK == last else s

    def weigh(n, x):
        span = slice(x - span_of(units[n][0])[0], x - span_of(units[n][0])[0] + BLOCK)
        weights[n % 2, :, span] = scaled(scores[n % 2, :, span] - tops[n]).astype(jnp.bfloat16)

    def gather(n):
        block, g = units[n]
        unit = block * 4 + g
        first, last, _ = span_of(block)
        v = kv[slot, 1, first:last, :]
        v = jnp.concatenate([v, jnp.ones((last - first, HEAD), jnp.bfloat16)], axis=1)
        o = jnp.dot(weights[n % 2, :, : last - first], v, preferred_element_type=jnp.float32)
        o, total = o[:, :HEAD], o[:, HEAD:]
        if part == "own":
            state[0][head, unit] = o
            state[1][head, unit] = total
            state[2][head, unit] = jnp.broadcast_to(tops[n], (BLOCK, HEAD))
            return
        if part == "before":
            fade = scaled(state[2][head, unit] - tops[n])
            o += fade * state[0][head, unit]
            total += fade * state[1][head, unit]
        out[place(block, g)] = (o / total).astype(jnp.bfloat16)

    for x in span_of(units[0][0])[2]:
        score(0, x)
    for n in range(len(units)):
        now = list(span_of(units[n][0])[2])
        later = list(span_of(units[n + 1][0])[2]) if n + 1 < len(units) else []
        for i in range(max(len(now), len(later))):
            if i < len(later):
                score(n + 1, later[i])
            if i < len(now):
                weigh(n, now[i])
        gather(n)
        if n == 3 and between:
            between()


def fill_bias(start_ref, bias):
    shard = lax.axis_index("seqa") * lax.axis_size("seqb") + lax.axis_index("seqb")
    for block in range(2):
        starts = []
        for r in range(2):
            row = start_ref[pl.ds(block * 2 + r, 1), :] - shard * ROWS
            row = jnp.broadcast_to(row.astype(jnp.float32), (HEAD, HEAD))
            starts.append(row.T)
        start = jnp.concatenate(starts, axis=0)
        for t in range(SPAN // HEAD):
            q_place = lax.broadcasted_iota(jnp.int32, (BLOCK, HEAD), 0) + block * BLOCK
            k_place = lax.broadcasted_iota(jnp.int32, (BLOCK, HEAD), 1) + (
                t * HEAD + block * BLOCK - 2 * ROWS
            )
            seen = (
                (k_place <= q_place)
                & (k_place > q_place - 2 * ROWS)
                & (k_place.astype(jnp.float32) >= start)
            )
            bias[block, :, t * HEAD : (t + 1) * HEAD] = jnp.where(
                seen, jnp.float32(3e38), jnp.float32(-1e30)
            )


def head_columns(h):
    return pl.ds(pl.multiple_of(h * 4 * HEAD, 4 * HEAD), 4 * HEAD)


def kernel(
    chips, q_hbm, k_hbm, v_hbm, start_ref, o_hbm, kv_last,
    q_ref, kv, hop, bias, scores, weights, acc, total, top, out,
    kv_sem, q_sem, o_sem, pad_sem, far_send, far_recv, near_send, near_recv,
    hop_send, hop_recv,
):
    heads = kv.shape[0]
    at = places(chips)
    own, one, two = slice(1024, 1536), slice(512, 1024), slice(0, 512)
    rounds = range(len(ROUND))
    late = [i for i in rounds if ROUND[i][0] == LAST]
    early = [i for i in rounds if ROUND[i][0] != LAST]
    (lone,) = {ROUND[i][0] for i in early}

    def load_kv(h, which):
        src = (k_hbm, v_hbm)[which]
        return pltpu.make_async_copy(
            src.at[:, pl.ds(h * HEAD, HEAD)], kv.at[h, which, own], kv_sem.at[h, which]
        )

    def load_q(h):
        columns = head_columns(h)
        return pltpu.make_async_copy(q_hbm.at[:, columns], q_ref.at[:, columns], q_sem.at[h])

    def store_o(h):
        columns = head_columns(h)
        return pltpu.make_async_copy(out.at[:, columns], o_hbm.at[:, columns], o_sem.at[h])

    def pad(h):
        dst = kv_last.at[:, two] if h is LAST else kv.at[h, :, two]
        return pltpu.make_async_copy(kv.at[h, :, own], dst, pad_sem.at[h])

    def sent(src, dst, sems, place):
        send, recv = sems
        return pltpu.make_async_remote_copy(
            src, dst, send, recv, device_id=at[place], device_id_type=MESH
        )

    def far(h):
        sems = far_send.at[h], far_recv.at[h]
        if h is LAST:
            return sent(kv.at[h, 1, own], kv_last.at[1, two], sems, "after")
        return sent(kv.at[h, :, own], kv.at[h, :, two], sems, "after")

    def near(h, src):
        sems = near_send.at[h], near_recv.at[h]
        if h is not LAST:
            return sent(kv.at[h, :, src], kv.at[h, :, one], sems, "partner")
        src = kv_last.at[:, src] if src is two else kv.at[h, :, src]
        return sent(src, kv_last.at[:, one], sems, "partner")

    def hops(stage, i):
        h, which = ROUND[i]
        sems = hop_send.at[stage, i], hop_recv.at[stage, i]
        if stage == 0:
            return sent(kv.at[h, which, own], hop.at[0, i], sems, "down")
        if stage == 1:
            return sent(hop.at[0, i], hop.at[1, i], sems, "down")
        dst = kv_last.at[which, two] if h is LAST else kv.at[h, which, two]
        return sent(hop.at[1, i], dst, sems, "last_to")

    def second(i):
        hops(0, i).wait_recv()
        hops(1, i).start()

    def third(i):
        hops(1, i).wait_recv()

        @pl.when(at["has_last_to"])
        def _():
            hops(2, i).start()

    order = [0, lone, LAST, *(h for h in range(1, LAST) if h != lone)]
    for h in order:
        for which in range(2):
            load_kv(h, which).start()
    for h in range(heads - 1):
        load_q(h).start()

    barrier = pltpu.get_barrier_semaphore()

    def ready(name):
        pl.semaphore_signal(barrier, inc=1, device_id=at[name], device_id_type=MESH)

    ready("partner")
    ready("up")

    @pl.when(at["has_before"])
    def _():
        ready("before")
        ready("last_from")

    pl.semaphore_wait(barrier, at["peers"])

    for h in order:
        for which in range(2):
            load_kv(h, which).wait()
        for i in rounds:
            if ROUND[i][0] == h:
                hops(0, i).start()

        @pl.when(at["has_after"])
        def _():
            if h not in (lone, LAST):
                far(h).start()

        @pl.when(at["core"] == 0)
        def _():
            near(h, own).start()

        @pl.when(jnp.logical_not(at["has_before"]))
        def _():
            pad(h).start()

    @pl.when(at["has_after"])
    def _():
        far(LAST).start()

    fill_bias(start_ref, bias)
    state = (acc, total, top)

    def first_step(h, carry):
        load_q(h).wait()
        attend(h, h, q_ref, kv, bias, scores, weights, state, out, (0, 1), "own")

        @pl.when(h == heads - 3)
        def _():
            second(0)
            second(1)

        return carry

    lax.fori_loop(0, heads - 1, first_step, 0)

    def step(h, carry):
        @pl.when(h == 0)
        def _():
            second(2)

        @pl.when(h == 2)
        def _():
            third(0)
            third(1)

        @pl.when(h == 3)
        def _():
            third(2)

        @pl.when(at["has_before"])
        def _():
            @pl.when(h != lone)
            def _():
                far(h).wait_recv()

            @pl.when(h == lone)
            def _():
                for i in early:
                    hops(2, i).wait_recv()

        @pl.when(jnp.logical_not(at["has_before"]))
        def _():
            pad(h).wait()

        @pl.when(at["core"] == 1)
        def _():
            near(h, two).start()

        near(h, own).wait_recv()
        work = q_ref, kv, bias, scores, weights, state, out
        if not isinstance(h, int):
            attend(h, h, *work, (0, 1), "before")
        else:
            attend(h, h, *work, (0,), "before")

            @pl.when(at["has_before"])
            def _():
                for i in late:
                    hops(2, i).wait_recv()
                far(LAST).wait_recv()

            @pl.when(jnp.logical_not(at["has_before"]))
            def _():
                pad(LAST).wait()

            @pl.when(at["core"] == 1)
            def _():
                near(LAST, two).start()

            attend(h, h, *work, (1,), "before")
        store_o(h).start()
        return carry

    lax.fori_loop(0, heads - 2, step, 0)
    step(heads - 2, 0)

    near(LAST, own).wait_recv()
    for h in range(heads):
        if h != LAST:
            store_o(h).wait()
        near(h, own).wait_send()
        if h != lone:

            @pl.when(at["has_after"])
            def _():
                far(h).wait_send()

    for i in rounds:
        hops(0, i).wait_send()
        hops(1, i).wait_send()

        @pl.when(at["has_last_to"])
        def _():
            hops(2, i).wait_send()


def finish(
    q_hbm, k_hbm, v_hbm, start_ref, first_hbm, kv_last, o_hbm,
    q_ref, kv, bias, scores, weights, out, kv_sem, q_sem, in_sem, o_sem,
):
    heads = k_hbm.shape[1] // HEAD
    columns = head_columns(LAST)
    loads = [
        pltpu.make_async_copy(kv_last, kv.at[0, :, : 2 * ROWS], kv_sem.at[0]),
        pltpu.make_async_copy(k_hbm.at[:, pl.ds(LAST * HEAD, HEAD)], kv.at[0, 0, 2 * ROWS :], kv_sem.at[1]),
        pltpu.make_async_copy(v_hbm.at[:, pl.ds(LAST * HEAD, HEAD)], kv.at[0, 1, 2 * ROWS :], kv_sem.at[2]),
        pltpu.make_async_copy(q_hbm.at[:, columns], q_ref, q_sem),
    ]
    takes = [
        pltpu.make_async_copy(first_hbm.at[:, head_columns(h)], out.at[h], in_sem.at[h])
        for h in range(heads - 1)
    ]
    stores = [
        pltpu.make_async_copy(out.at[h], o_hbm.at[:, head_columns(h)], o_sem.at[h])
        for h in range(heads - 1)
    ]
    halves = [
        pltpu.make_async_copy(
            out.at[LAST, pl.ds(block * BLOCK, BLOCK)],
            o_hbm.at[pl.ds(block * BLOCK, BLOCK), columns],
            o_sem.at[LAST + block],
        )
        for block in range(2)
    ]
    for copy in loads:
        copy.start()
    fill_bias(start_ref, bias)
    for copy in loads:
        copy.wait()
    for copy in takes:
        copy.start()

    def between():
        halves[0].start()
        for h in range(heads - 1):
            takes[h].wait()
            stores[h].start()

    attend(0, 0, q_ref, kv, bias, scores, weights, None, out.at[LAST], (0, 1), "all", between)
    halves[1].start()
    for copy in stores + halves:
        copy.wait()


def local(queries, keys, values, doc_start):
    heads = keys.shape[1] // HEAD
    chips = lax.axis_size("seqa") * lax.axis_size("seqb") // 2
    anywhere = pl.BlockSpec(memory_space=pl.ANY)
    held = pl.BlockSpec(memory_space=pltpu.VMEM)
    dma = pltpu.SemaphoreType.DMA
    starts = doc_start.reshape(ROWS // HEAD, HEAD)
    work = [
        pltpu.VMEM((2, BLOCK, SPAN), jnp.float32),
        pltpu.VMEM((2, BLOCK, SPAN), jnp.float32),
        pltpu.VMEM((2, BLOCK, SPAN), jnp.bfloat16),
    ]
    first, kv_last = pl.pallas_call(
        functools.partial(kernel, chips),
        out_shape=(
            jax.ShapeDtypeStruct(queries.shape, queries.dtype),
            jax.ShapeDtypeStruct((2, 2 * ROWS, HEAD), keys.dtype),
        ),
        in_specs=[anywhere] * 3 + [held],
        out_specs=(anywhere, anywhere),
        scratch_shapes=[
            pltpu.VMEM(queries.shape, jnp.bfloat16),
            pltpu.VMEM((heads, 2, 3 * ROWS, HEAD), jnp.bfloat16),
            pltpu.VMEM((2, len(ROUND), ROWS, HEAD), jnp.bfloat16),
            *work,
            *[pltpu.VMEM((heads - 1, 8, BLOCK, HEAD), jnp.float32)] * 3,
            pltpu.VMEM(queries.shape, jnp.bfloat16),
            dma((heads, 2)), dma((heads,)), dma((heads,)), dma((heads,)),
            dma((heads,)), dma((heads,)), dma((heads,)), dma((heads,)),
            dma((3, len(ROUND))), dma((3, len(ROUND))),
        ],
        compiler_params=pltpu.CompilerParams(
            collective_id=0, has_side_effects=True, vmem_limit_bytes=60 * 2**20
        ),
        name="attention",
    )(queries, keys, values, starts)
    return pl.pallas_call(
        finish,
        out_shape=jax.ShapeDtypeStruct(queries.shape, queries.dtype),
        in_specs=[anywhere] * 3 + [held] + [anywhere] * 2,
        out_specs=anywhere,
        scratch_shapes=[
            pltpu.VMEM((ROWS, 4 * HEAD), jnp.bfloat16),
            pltpu.VMEM((1, 2, 3 * ROWS, HEAD), jnp.bfloat16),
            *work,
            pltpu.VMEM((heads, ROWS, 4 * HEAD), jnp.bfloat16),
            dma((3,)), dma, dma((heads,)), dma((heads + 1,)),
        ],
        compiler_params=pltpu.CompilerParams(vmem_limit_bytes=60 * 2**20),
        name="finish",
    )(queries, keys, values, starts, first, kv_last)


def solution(mesh):
    shards = P(("seqa", "seqb"), None)
    return jax.shard_map(
        local,
        mesh=mesh,
        in_specs=(shards, shards, shards, P(("seqa", "seqb"))),
        out_specs=shards,
        check_vma=False,
    )
```

time: 65.5 us -> 57.4 us (0.88)
  the two profiles are of different devices: /device:TPU:102 before, /device:TPU:4 now
where the time goes in v2:
time: 57.4 us; the launch traced here: 57.2 us
  Pallas kernels  57.2 us (100%)
    pallas_call x1, Pallas kernels, local(): pl.pallas_call(functools.partial(kernel, chips), out_shape=(jax.ShapeDtyp...  50.3 us
    pallas_call x1, Pallas kernels, local(): pl.pallas_call(finish, out_shape=jax.ShapeDtypeStruct(queries.shape, quer...  6.86 us

profile of v2, /device:TPU:4, one launch (start us, length us, event | category | flops | bytes accessed | tf_op | source)
XLA Modules:
  0.0 57.2 jit_solution(12056159513190815935)
XLA Ops:
  0.0 50.3 %attention.1 = (bf16[512,4096]{1,0:T(8,128)(2,1)}, bf16[2,1024,128]{2,1,0:T(8,128)(2,1)}) custom-call(bf16[512,4096]{1,0:T(8,128)(2,1)} %q_hbm.3, bf16[512,1024]{1,0:T(8,128)(2,1)} %k_hbm.3, bf16[512,1024]{1,0:T(8,128)(2,1)} %v_hbm.3, s32[4,128]{1,0:T(4,128)} %bitcast.1), custom_call_target="tpu_custom_call" | custom-call | tf_op jit(solution)/shard_map/attention/pallas_call | solution.py:427
  50.4 6.9 %finish.1 = bf16[512,4096]{1,0:T(8,128)(2,1)} custom-call(bf16[512,4096]{1,0:T(8,128)(2,1)} %q_hbm.3, bf16[512,1024]{1,0:T(8,128)(2,1)} %k_hbm.3, bf16[512,1024]{1,0:T(8,128)(2,1)} %v_hbm.3, s32[4,128]{1,0:T(4,128)} %bitcast.2, bf16[512,4096]{1,0:T(8,128)(2,1)} %get-tuple-element.7.first_hbm, bf16[2,1024,128]{2,1,0:T(8,128)(2,1)} %get-tuple-element.8.kv_last), custom_call_target="tpu_custom_call" | custom-call | tf_op jit(solution)/shard_map/finish/pallas_call | solution.py:451

commit v3 on v2

--- a/solution.py
+++ b/solution.py
@@ -14,7 +14,8 @@
 BLOCK = 256
 SPAN = 5 * BLOCK
 SCALE = math.log2(math.e) / math.sqrt(HEAD)
-ROUND = ((4, 0), (4, 1), (7, 0))
+ROUND = ((4, 0, 512), (4, 1, 512), (6, 0, 512), (6, 1, 256))
+SPLIT = 6
 LAST = 7
 COLUMN = 4
 
@@ -159,9 +160,8 @@
     at = places(chips)
     own, one, two = slice(1024, 1536), slice(512, 1024), slice(0, 512)
     rounds = range(len(ROUND))
-    late = [i for i in rounds if ROUND[i][0] == LAST]
-    early = [i for i in rounds if ROUND[i][0] != LAST]
-    (lone,) = {ROUND[i][0] for i in early}
+    detour = sorted({h for h, _, _ in ROUND} - {SPLIT})
+    cut = ROUND[-1][2]
 
     def load_kv(h, which):
         src = (k_hbm, v_hbm)[which]
@@ -177,9 +177,14 @@
         columns = head_columns(h)
         return pltpu.make_async_copy(out.at[:, columns], o_hbm.at[:, columns], o_sem.at[h])
 
-    def pad(h):
-        dst = kv_last.at[:, two] if h is LAST else kv.at[h, :, two]
-        return pltpu.make_async_copy(kv.at[h, :, own], dst, pad_sem.at[h])
+    def pad(h, which):
+        src = (k_hbm, v_hbm)[which]
+        return pltpu.make_async_copy(
+            src.at[:, pl.ds(h * HEAD, HEAD)], kv.at[h, which, two], pad_sem.at[h, which]
+        )
+
+    def save():
+        return pltpu.make_async_copy(kv.at[LAST, :, two], kv_last.at[:, two], o_sem.at[LAST])
 
     def sent(src, dst, sems, place):
         send, recv = sems
@@ -189,26 +194,23 @@
 
     def far(h):
         sems = far_send.at[h], far_recv.at[h]
-        if h is LAST:
-            return sent(kv.at[h, 1, own], kv_last.at[1, two], sems, "after")
+        if h is SPLIT:
+            src = kv.at[h, 1, own.start + cut : own.stop]
+            return sent(src, kv.at[h, 1, two.start + cut : two.stop], sems, "after")
         return sent(kv.at[h, :, own], kv.at[h, :, two], sems, "after")
 
     def near(h, src):
         sems = near_send.at[h], near_recv.at[h]
-        if h is not LAST:
-            return sent(kv.at[h, :, src], kv.at[h, :, one], sems, "partner")
-        src = kv_last.at[:, src] if src is two else kv.at[h, :, src]
-        return sent(src, kv_last.at[:, one], sems, "partner")
+        dst = kv_last.at[:, one] if h is LAST else kv.at[h, :, one]
+        return sent(kv.at[h, :, src], dst, sems, "partner")
 
     def hops(stage, i):
-        h, which = ROUND[i]
+        h, which, rows = ROUND[i]
         sems = hop_send.at[stage, i], hop_recv.at[stage, i]
-        if stage == 0:
-            return sent(kv.at[h, which, own], hop.at[0, i], sems, "down")
-        if stage == 1:
-            return sent(hop.at[0, i], hop.at[1, i], sems, "down")
-        dst = kv_last.at[which, two] if h is LAST else kv.at[h, which, two]
-        return sent(hop.at[1, i], dst, sems, "last_to")
+        src = kv.at[h, which, own.start : own.start + rows]
+        stops = src, hop.at[0, i, :rows], hop.at[1, i, :rows], kv.at[h, which, two.start : two.start + rows]
+        place = "last_to" if stage == 2 else "down"
+        return sent(stops[stage], stops[stage + 1], sems, place)
 
     def second(i):
         hops(0, i).wait_recv()
@@ -221,7 +223,7 @@
         def _():
             hops(2, i).start()
 
-    order = [0, lone, LAST, *(h for h in range(1, LAST) if h != lone)]
+    order = [0, *detour, SPLIT, *(h for h in range(1, heads) if h not in (*detour, SPLIT))]
     for h in order:
         for which in range(2):
             load_kv(h, which).start()
@@ -252,7 +254,7 @@
 
         @pl.when(at["has_after"])
         def _():
-            if h not in (lone, LAST):
+            if h not in (*detour, SPLIT, LAST):
                 far(h).start()
 
         @pl.when(at["core"] == 0)
@@ -261,10 +263,12 @@
 
         @pl.when(jnp.logical_not(at["has_before"]))
         def _():
-            pad(h).start()
+            for which in range(2):
+                pad(h, which).start()
 
     @pl.when(at["has_after"])
     def _():
+        far(SPLIT).start()
         far(LAST).start()
 
     fill_bias(start_ref, bias)
@@ -287,30 +291,38 @@
         @pl.when(h == 0)
         def _():
             second(2)
-
-        @pl.when(h == 2)
-        def _():
-            third(0)
-            third(1)
-
-        @pl.when(h == 3)
-        def _():
-            third(2)
+            second(3)
+
+        for i in rounds:
+
+            @pl.when(h == 2 + i // 2)
+            def _():
+                third(i)
 
         @pl.when(at["has_before"])
         def _():
-            @pl.when(h != lone)
+            direct = True
+            if isinstance(h, int):
+                for i in rounds:
+                    if ROUND[i][0] == SPLIT:
+                        hops(2, i).wait_recv()
+            for d in detour:
+                direct &= h != d
+
+                @pl.when(h == d)
+                def _():
+                    for i in rounds:
+                        if ROUND[i][0] == d:
+                            hops(2, i).wait_recv()
+
+            @pl.when(direct)
             def _():
                 far(h).wait_recv()
 
-            @pl.when(h == lone)
-            def _():
-                for i in early:
-                    hops(2, i).wait_recv()
-
         @pl.when(jnp.logical_not(at["has_before"]))
         def _():
-            pad(h).wait()
+            for which in range(2):
+                pad(h, which).wait()
 
         @pl.when(at["core"] == 1)
         def _():
@@ -325,31 +337,32 @@
 
             @pl.when(at["has_before"])
             def _():
-                for i in late:
-                    hops(2, i).wait_recv()
                 far(LAST).wait_recv()
 
             @pl.when(jnp.logical_not(at["has_before"]))
             def _():
-                pad(LAST).wait()
+                for which in range(2):
+                    pad(LAST, which).wait()
 
             @pl.when(at["core"] == 1)
             def _():
                 near(LAST, two).start()
 
+            save().start()
             attend(h, h, *work, (1,), "before")
         store_o(h).start()
         return carry
 
     lax.fori_loop(0, heads - 2, step, 0)
-    step(heads - 2, 0)
+    step(SPLIT, 0)
 
     near(LAST, own).wait_recv()
+    save().wait()
     for h in range(heads):
         if h != LAST:
             store_o(h).wait()
         near(h, own).wait_send()
-        if h != lone:
+        if h not in detour:
 
             @pl.when(at["has_after"])
             def _():
@@ -439,7 +452,7 @@
             *work,
             *[pltpu.VMEM((heads - 1, 8, BLOCK, HEAD), jnp.float32)] * 3,
             pltpu.VMEM(queries.shape, jnp.bfloat16),
-            dma((heads, 2)), dma((heads,)), dma((heads,)), dma((heads,)),
+            dma((heads, 2)), dma((heads,)), dma((heads,)), dma((heads, 2)),
             dma((heads,)), dma((heads,)), dma((heads,)), dma((heads,)),
             dma((3, len(ROUND))), dma((3, len(ROUND))),
         ],

time: 57.4 us -> 56.7 us (0.988); the launches traced: 57.2 us -> 55.8 us
  Pallas kernels: 57.2 us -> 55.8 us
    pallas_call x1, Pallas kernels: 50.3 us -> 49 us  [local(): pl.pallas_call(functools.partial(kernel, chips), out_shape=(jax.ShapeDtyp...]
where the time goes in v3:
time: 56.7 us; the launch traced here: 55.8 us
  Pallas kernels  55.8 us (98%)
    pallas_call x1, Pallas kernels, local(): pl.pallas_call(functools.partial(kernel, chips), out_shape=(jax.ShapeDtyp...  49 us
    pallas_call x1, Pallas kernels, local(): pl.pallas_call(finish, out_shape=jax.ShapeDtypeStruct(queries.shape, quer...  6.87 us

profile of v3, /device:TPU:4, one launch (start us, length us, event | category | flops | bytes accessed | tf_op | source)
XLA Modules:
  0.0 55.8 jit_solution(5386882159636624543)
XLA Ops:
  0.0 49.0 %attention.1 = (bf16[512,4096]{1,0:T(8,128)(2,1)}, bf16[2,1024,128]{2,1,0:T(8,128)(2,1)}) custom-call(bf16[512,4096]{1,0:T(8,128)(2,1)} %q_hbm.3, bf16[512,1024]{1,0:T(8,128)(2,1)} %k_hbm.3, bf16[512,1024]{1,0:T(8,128)(2,1)} %v_hbm.3, s32[4,128]{1,0:T(4,128)} %bitcast.1), custom_call_target="tpu_custom_call" | custom-call | tf_op jit(solution)/shard_map/attention/pallas_call | solution.py:440
  49.0 6.9 %finish.1 = bf16[512,4096]{1,0:T(8,128)(2,1)} custom-call(bf16[512,4096]{1,0:T(8,128)(2,1)} %q_hbm.3, bf16[512,1024]{1,0:T(8,128)(2,1)} %k_hbm.3, bf16[512,1024]{1,0:T(8,128)(2,1)} %v_hbm.3, s32[4,128]{1,0:T(4,128)} %bitcast.2, bf16[512,4096]{1,0:T(8,128)(2,1)} %get-tuple-element.7.first_hbm, bf16[2,1024,128]{2,1,0:T(8,128)(2,1)} %get-tuple-element.8.kv_last), custom_call_target="tpu_custom_call" | custom-call | tf_op jit(solution)/shard_map/finish/pallas_call | solution.py:464
